TPU v7x, 256 devices: a whole 4x4x8 slice. The times are simulated.
256 devices in a mesh: mission: 8 (over x, z_lo), arc: 32 (over z_hi, y, core).
Axes of the slice: x: 4, y: 4, z: 8 (z_hi: 4, z_lo: 2; z = z_hi * 2 + z_lo), core: 2. Of those that a mesh axis runs over, the one named last changes fastest.
Arguments:
- design: bfloat16 [20480, 5120], P(('mission', 'arc')), may hold values from -3 to 3
- nuisance_design: bfloat16 [20480, 128], P(('mission', 'arc')), may hold values from -1 to 1
- observed: float32 [20480], P(('mission', 'arc')), may hold values from -6 to 6
- arc_of_row: int32 [20480], P(('mission', 'arc')), may hold values from 0 to 1, as said below
- nuis_size: int32 [512], P(('mission', 'arc')), may hold values from 32 to 128
- weight_index: int32 [20480], P(('mission', 'arc')), may hold values from 0 to 7
- kind_weight: float32 [8], replicated, may hold values from 0.3 to 3
- mission_weight: float32 [8], P('mission'), may hold values from 0.3 to 3
Outputs:
- normal_fold: float32 [2560, 5120], P(('mission', 'arc'))
- right_side: float32 [5120], P(('mission', 'arc'))
- tail_diagonal: float32 [2560], P(('mission', 'arc'))
Inputs may be any that keep to these rules, and one draw needn't show every extreme that they name: `arc_of_row`: in each row block of 80 rows the rows of arc 0 come first and those of arc 1 follow; each arc has at least 20 rows.
All inputs are finite; a program needn't handle non-finite values.
Results may differ from a plain program's by a relative error of at most 0.019.
Values may be sent and summed in bfloat16 or wider, within the bound.
A program may use at most 192 MiB of HBM per device.

v0:
```python
import jax
import jax.numpy as jnp
from jax import lax
from jax.sharding import PartitionSpec as P

ARCS_DEV = 2


def local_system(
    design, nuisance_design, observed, arc_of_row, nuis_size, weight_index, kind_weight
):
    kind_ids = jnp.arange(kind_weight.shape[0], dtype=jnp.int32)
    row_weight = jnp.sum(
        jnp.where(weight_index[:, None] == kind_ids[None, :], kind_weight[None, :], 0.0), axis=1
    )
    nuis_ids = jnp.arange(nuisance_design.shape[1], dtype=jnp.int32)
    eye_block = jnp.eye(nuisance_design.shape[1], dtype=jnp.float32)
    blocks = []
    solved = []
    solved_obs = []
    for arc_id in range(ARCS_DEV):
        col_mask = (nuis_ids < nuis_size[arc_id]).astype(jnp.bfloat16)
        in_arc = (arc_of_row == arc_id).astype(jnp.float32)
        masked = nuisance_design * col_mask[None, :]
        weighted = (masked.astype(jnp.float32) * (row_weight * in_arc)[:, None]).astype(
            jnp.bfloat16
        )
        normal_ll = jnp.dot(weighted.T, masked, preferred_element_type=jnp.float32) + eye_block
        coupling = jnp.dot(weighted.T, design, preferred_element_type=jnp.float32)
        obs_part = jnp.dot(weighted.T.astype(jnp.float32), observed)
        factor = jnp.linalg.cholesky(normal_ll)
        blocks.append(weighted)
        solved.append(jax.scipy.linalg.cho_solve((factor, True), coupling).astype(jnp.bfloat16))
        solved_obs.append(jax.scipy.linalg.cho_solve((factor, True), obs_part))
    stacked = jnp.concatenate(blocks, axis=1)
    solved_all = jnp.concatenate(solved, axis=0)
    obs_all = jnp.concatenate(solved_obs, axis=0)
    reduced = (
        row_weight[:, None] * design.astype(jnp.float32)
        - jnp.dot(stacked, solved_all, preferred_element_type=jnp.float32)
    ).astype(jnp.bfloat16)
    reduced_obs = (row_weight * observed - jnp.dot(stacked.astype(jnp.float32), obs_all)).astype(
        jnp.bfloat16
    )
    right_term = jnp.dot(reduced_obs, design, preferred_element_type=jnp.float32)
    half_width = design.shape[1] // 2
    tail_term = jnp.sum(
        design[:, half_width:].astype(jnp.float32) * reduced[:, half_width:].astype(jnp.float32),
        axis=0,
    )
    return (reduced, right_term, tail_term)


def on_device(
    design,
    nuisance_design,
    observed,
    arc_of_row,
    nuis_size,
    weight_index,
    kind_weight,
    mission_weight,
):
    reduced, right_term, tail_term = local_system(
        design, nuisance_design, observed, arc_of_row, nuis_size, weight_index, kind_weight
    )
    weight = mission_weight[0]
    width_all = design.shape[1]
    half_width = width_all // 2
    groups = lax.axis_size("mission")
    members = lax.axis_size("arc")
    final_rows = half_width // (groups * members)
    mirrored = design[:, ::-1]
    reduced_mirror = reduced[:, ::-1]
    row_numbers = jnp.arange(half_width, dtype=jnp.int32)

    def permute(matrix):
        shaped = matrix.reshape(matrix.shape[0], groups, members, final_rows)
        return jnp.transpose(shaped, (0, 2, 1, 3)).reshape(matrix.shape[0], half_width)

    cols_above = permute(design[:, :half_width])
    cols_mirror = permute(mirrored[:, :half_width])
    row_order = permute(row_numbers[None, :])[0]
    columns = jnp.arange(width_all, dtype=jnp.int32)
    contract_dims = (((0,), (0,)), ((), ()))
    tile_cols = 512
    tile_count = width_all // tile_cols

    def fold_rows():
        block_rows = lax.axis_size("arc") * (half_width // members)
        while block_rows > 640 and block_rows % 2 == 0:
            block_rows = block_rows // 2

        def one_block(block_id):
            block_start = block_id * block_rows
            above_cols = lax.dynamic_slice_in_dim(cols_above, block_start, block_rows, 1)
            mirror_cols = lax.dynamic_slice_in_dim(cols_mirror, block_start, block_rows, 1)
            rows_here = lax.dynamic_slice_in_dim(row_order, block_start, block_rows, 0)
            low_row = jnp.min(rows_here)
            high_row = jnp.max(rows_here)
            pieces = []
            for tile_id in range(tile_count):
                col_start = tile_id * tile_cols
                above_tile = reduced[:, col_start : col_start + tile_cols]
                mirror_tile = reduced_mirror[:, col_start : col_start + tile_cols]
                tile_ids = columns[col_start : col_start + tile_cols]

                def above_only():
                    return lax.dot_general(
                        above_cols, above_tile, contract_dims, preferred_element_type=jnp.float32
                    )

                def mirror_only():
                    return lax.dot_general(
                        mirror_cols, mirror_tile, contract_dims, preferred_element_type=jnp.float32
                    )

                def mixed_tile():
                    return jnp.where(
                        tile_ids[None, :] >= rows_here[:, None], above_only(), mirror_only()
                    )

                tile_kind = jnp.where(
                    col_start >= high_row, 0, jnp.where(col_start + tile_cols <= low_row, 1, 2)
                ).astype(jnp.int32)
                pieces.append(lax.switch(tile_kind, [above_only, mirror_only, mixed_tile]))
            return weight * jnp.concatenate(pieces, axis=1)

        stacked_pieces = lax.map(
            one_block,
            jnp.arange(
                lax.axis_size("arc") * (half_width // members) // block_rows, dtype=jnp.int32
            ),
        )
        return stacked_pieces.reshape(lax.axis_size("arc") * (half_width // members), width_all)

    partial_fold = lax.psum_scatter(
        fold_rows().astype(jnp.bfloat16), "arc", scatter_dimension=0, tiled=True
    )
    normal_fold = lax.psum_scatter(partial_fold, "mission", scatter_dimension=0, tiled=True).astype(
        jnp.float32
    )
    right_side, tail_diagonal = (
        lax.psum_scatter(weight * right_term, ("mission", "arc"), scatter_dimension=0, tiled=True),
        lax.psum_scatter(weight * tail_term, ("mission", "arc"), scatter_dimension=0, tiled=True),
    )
    return (normal_fold, right_side, tail_diagonal)


def solution(mesh):
    placed = (
        P(("mission", "arc"), None),
        P(("mission", "arc"), None),
        P(("mission", "arc")),
        P(("mission", "arc")),
        P(("mission", "arc")),
        P(("mission", "arc")),
        P(),
        P("mission"),
    )
    return jax.shard_map(
        on_device,
        mesh=mesh,
        in_specs=placed,
        out_specs=(P(("mission", "arc"), None), P(("mission", "arc")), P(("mission", "arc"))),
        check_vma=False,
    )
```

profile of v0, /device:TPU:6, one launch (start us, length us, event | category | flops | bytes accessed | tf_op | source)
XLA Modules:
  0.0 665.5 jit_solution(10079454155274101493)
XLA Ops:
  20.5 11.7 %cholesky.44 = f32[128,128]{1,0:T(8,128)S(1)} custom-call(f32[128,128]{1,0:T(8,128)S(1)} %fusion.33), custom_call_target="Cholesky" | custom-call | tf_op jit(solution)/shard_map/jit(cholesky)/cholesky | solution.py:31
  33.6 9.8 %custom-call.14 = f32[1,128,128]{1,2,0:T(8,128)S(1)} custom-call(f32[1,128,128]{2,1,0:T(8,128)S(1)} %fusion.20), custom_call_target="InvertDiagBlocksLowerTriangular" | custom-call | tf_op jit(solution)/shard_map/jit(_cho_solve)/triangular_solve | solution.py:33
  43.5 11.7 %cholesky.55 = f32[128,128]{1,0:T(8,128)S(1)} custom-call(f32[128,128]{1,0:T(8,128)S(1)} %fusion.27), custom_call_target="Cholesky" | custom-call | tf_op jit(solution)/shard_map/jit(cholesky)/cholesky | solution.py:31
  56.6 10.0 %custom-call.15 = f32[1,128,128]{1,2,0:T(8,128)S(1)} custom-call(f32[1,128,128]{2,1,0:T(8,128)S(1)} %fusion.21), custom_call_target="InvertDiagBlocksLowerTriangular" | custom-call | tf_op jit(solution)/shard_map/jit(_cho_solve)/triangular_solve | solution.py:33
  75.8 4.1 fusion.31
  80.0 2.4 convolution_convert_fusion.1
  82.4 2.5 fusion.25
  84.9 2.4 convolution_convert_fusion
  87.9 3.7 rev.4
  91.6 258.8 %while.12 = (s32[]{:T(128)}, bf16[4,640,5120]{2,1,0:T(8,128)(2,1)}, f32[]{:T(128)}, s32[4]{0:T(128)S(1)}, s32[2560]{0:T(1024)S(1)}, /*index=5*/bf16[80,2560]{1,0...) while((s32[]{:T(128)}, bf16[4,640,5120]{2,1,0:T(8,128)(2,1)}, ...), condition=%wide.region_36.39_spmd.clone.clone, body=%wide.region_3.38_spmd.clone.clone.sunk | while | flops 1058407680 | bytes 157238096 | solution.py:129
  119.9 2.4 conditional.47
  126.9 2.7 conditional.44
  136.8 2.6 constant_dynamic-update-slice_fusion.20
  153.8 9.8 %multiply_dynamic-update-slice_fusion.2 = bf16[4,640,5120]{2,1,0:T(8,128)(2,1)} fusion(bf16[4,640,5120]{2,1,0:T(8,128)(2,1)} %get-tuple-element.709, s32[]{:T(128)S(6)} %copy.91, f32[1,640,5120]{2,1,0:T(8,128)} %constant_dynamic-update-slice_fusion.29, f32[]{:T(128)} %get-tuple-element.733), kind=kLoop, calls=%fused_computation.41.clone.1 | loop fusion | flops 3276800 | bytes 26214916 | tf_op jit(solution)/shard_map/while/body/jit(dynamic_update_index_in_dim)/dynamic_update_slice | solution.py:129
  182.1 2.4 conditional.47
  182.1 2.4 convolution_bitcast_fusion.14
  189.1 2.7 conditional.44
  199.0 2.6 constant_dynamic-update-slice_fusion.20
  216.1 9.9 %multiply_dynamic-update-slice_fusion.2 = bf16[4,640,5120]{2,1,0:T(8,128)(2,1)} fusion(bf16[4,640,5120]{2,1,0:T(8,128)(2,1)} %get-tuple-element.709, s32[]{:T(128)S(6)} %copy.91, f32[1,640,5120]{2,1,0:T(8,128)} %constant_dynamic-update-slice_fusion.29, f32[]{:T(128)} %get-tuple-element.733), kind=kLoop, calls=%fused_computation.41.clone.1 | loop fusion | flops 3276800 | bytes 26214916 | tf_op jit(solution)/shard_map/while/body/jit(dynamic_update_index_in_dim)/dynamic_update_slice | solution.py:129
  244.4 2.4 conditional.47
  244.4 2.4 convolution_bitcast_fusion.14
  251.4 2.7 conditional.44
  261.3 2.6 constant_dynamic-update-slice_fusion.20
  278.3 9.8 %multiply_dynamic-update-slice_fusion.2 = bf16[4,640,5120]{2,1,0:T(8,128)(2,1)} fusion(bf16[4,640,5120]{2,1,0:T(8,128)(2,1)} %get-tuple-element.709, s32[]{:T(128)S(6)} %copy.91, f32[1,640,5120]{2,1,0:T(8,128)} %constant_dynamic-update-slice_fusion.29, f32[]{:T(128)} %get-tuple-element.733), kind=kLoop, calls=%fused_computation.41.clone.1 | loop fusion | flops 3276800 | bytes 26214916 | tf_op jit(solution)/shard_map/while/body/jit(dynamic_update_index_in_dim)/dynamic_update_slice | solution.py:129
  306.5 2.4 conditional.47
  306.5 2.4 convolution_bitcast_fusion.14
  313.5 2.7 conditional.44
  323.4 2.6 constant_dynamic-update-slice_fusion.20
  340.5 9.8 %multiply_dynamic-update-slice_fusion.2 = bf16[4,640,5120]{2,1,0:T(8,128)(2,1)} fusion(bf16[4,640,5120]{2,1,0:T(8,128)(2,1)} %get-tuple-element.709, s32[]{:T(128)S(6)} %copy.91, f32[1,640,5120]{2,1,0:T(8,128)} %constant_dynamic-update-slice_fusion.29, f32[]{:T(128)} %get-tuple-element.733), kind=kLoop, calls=%fused_computation.41.clone.1 | loop fusion | flops 3276800 | bytes 26214916 | tf_op jit(solution)/shard_map/while/body/jit(dynamic_update_index_in_dim)/dynamic_update_slice | solution.py:129
  352.2 220.3 %reduce-scatter.2.cloned.1.call-done = bf16[80,5120]{1,0:T(8,128)(2,1)} async-done(((bf16[2560,5120]{1,0:T(8,128)(2,1)}), bf16[80,5120]{1,0:T(8,128)(2,1)}) %reduce-scatter.2.cloned.1.call-update) | async-done | bytes 819216 | tf_op jit(solution)/shard_map/reduce_scatter | solution.py:137
  575.1 75.0 %all-reduce.3 = (f32[5120]{0:T(1024)S(1)}, f32[2560]{0:T(1024)S(1)}) all-reduce(f32[5120]{0:T(1024)S(1)} %broadcast_multiply_fusion, f32[2560]{0:T(1024)S(1)} %broadcast_multiply_fusion.1), channel_id=4, replica_groups=mesh['mission'=8,'arc'=32] {'mission','arc'}, use_global_device_ids=true, to_apply=%region_39.43.clone | all-reduce | flops 7680 | bytes 61440
  651.3 5.5 all-reduce.6.cloned.1.call-done
  (404 shorter events, 221.4 us)
Async XLA Ops:
  7.2 565.4 %reduce-scatter.2.cloned.1.call-start = ((), (), s32[]{:S(2)}) async-start(), calls=%async_computation.1 | async-start | bytes 27033600 | tf_op jit(solution)/shard_map/reduce_scatter | solution.py:137
  9.3 77.9 %copy-start.42 = (f32[80]{0:T(128)}, f32[80]{0:T(128)S(1)}, u32[]{:S(2)}) copy-start(f32[80]{0:T(128)S(1)} %select_reduce_fusion.2) | copy-start | bytes 964
  13.2 74.1 %copy-start.30 = (bf16[80,128]{1,0:T(8,128)(2,1)}, bf16[80,128]{1,0:T(8,128)(2,1)S(1)}, u32[]{:S(2)}) copy-start(bf16[80,128]{1,0:T(8,128)(2,1)S(1)} %get-tuple-element.572) | copy-start | bytes 61444
  13.2 74.1 %copy-start.32 = (bf16[80,128]{1,0:T(8,128)(2,1)}, bf16[80,128]{1,0:T(8,128)(2,1)S(1)}, u32[]{:S(2)}) copy-start(bf16[80,128]{1,0:T(8,128)(2,1)S(1)} %get-tuple-element.573) | copy-start | bytes 61444
  43.4 36.6 %copy-start.26 = (f32[1,128,128]{1,2,0:T(8,128)}, f32[1,128,128]{1,2,0:T(8,128)S(1)}, u32[]{:S(2)}) copy-start(f32[1,128,128]{1,2,0:T(8,128)S(1)} %custom-call.14) | copy-start | bytes 196612
  66.6 18.3 %copy-start.24 = (f32[1,128,128]{1,2,0:T(8,128)}, f32[1,128,128]{1,2,0:T(8,128)S(1)}, u32[]{:S(2)}) copy-start(f32[1,128,128]{1,2,0:T(8,128)S(1)} %custom-call.15) | copy-start | bytes 196612
  101.5 15.2 %copy-start.19 = (bf16[80,2560]{1,0:T(8,128)(2,1)}, bf16[80,2560]{1,0:T(8,128)(2,1)S(1)}, u32[]{:S(2)}) copy-start(bf16[80,2560]{1,0:T(8,128)(2,1)S(1)} %get-tuple-element.738) | copy-start | bytes 1228804 | tf_op jit(solution)/shard_map/while
  101.5 15.2 %copy-start.21 = (bf16[80,2560]{1,0:T(8,128)(2,1)}, bf16[80,2560]{1,0:T(8,128)(2,1)S(1)}, u32[]{:S(2)}) copy-start(bf16[80,2560]{1,0:T(8,128)(2,1)S(1)} %get-tuple-element.736) | copy-start | bytes 1228804 | tf_op jit(solution)/shard_map/while
  101.5 16.7 %copy-start.7 = (bf16[80,5120]{1,0:T(8,128)(2,1)}, bf16[80,5120]{1,0:T(8,128)(2,1)S(1)}, u32[]{:S(2)}) copy-start(bf16[80,5120]{1,0:T(8,128)(2,1)S(1)} %get-tuple-element.737) | copy-start | bytes 2457604 | tf_op jit(solution)/shard_map/while
  101.5 16.7 %copy-start.9 = (bf16[80,5120]{1,0:T(8,128)(2,1)}, bf16[80,5120]{1,0:T(8,128)(2,1)S(1)}, u32[]{:S(2)}) copy-start(bf16[80,5120]{1,0:T(8,128)(2,1)S(1)} %get-tuple-element.739) | copy-start | bytes 2457604 | tf_op jit(solution)/shard_map/while
  163.7 15.2 %copy-start.19 = (bf16[80,2560]{1,0:T(8,128)(2,1)}, bf16[80,2560]{1,0:T(8,128)(2,1)S(1)}, u32[]{:S(2)}) copy-start(bf16[80,2560]{1,0:T(8,128)(2,1)S(1)} %get-tuple-element.738) | copy-start | bytes 1228804 | tf_op jit(solution)/shard_map/while
  163.7 15.2 %copy-start.21 = (bf16[80,2560]{1,0:T(8,128)(2,1)}, bf16[80,2560]{1,0:T(8,128)(2,1)S(1)}, u32[]{:S(2)}) copy-start(bf16[80,2560]{1,0:T(8,128)(2,1)S(1)} %get-tuple-element.736) | copy-start | bytes 1228804 | tf_op jit(solution)/shard_map/while
  163.7 16.7 %copy-start.7 = (bf16[80,5120]{1,0:T(8,128)(2,1)}, bf16[80,5120]{1,0:T(8,128)(2,1)S(1)}, u32[]{:S(2)}) copy-start(bf16[80,5120]{1,0:T(8,128)(2,1)S(1)} %get-tuple-element.737) | copy-start | bytes 2457604 | tf_op jit(solution)/shard_map/while
  163.7 16.7 %copy-start.9 = (bf16[80,5120]{1,0:T(8,128)(2,1)}, bf16[80,5120]{1,0:T(8,128)(2,1)S(1)}, u32[]{:S(2)}) copy-start(bf16[80,5120]{1,0:T(8,128)(2,1)S(1)} %get-tuple-element.739) | copy-start | bytes 2457604 | tf_op jit(solution)/shard_map/while
  216.0 9.9 %copy-start.8 = (bf16[80,5120]{1,0:T(8,128)(2,1)S(1)}, bf16[80,5120]{1,0:T(8,128)(2,1)}, u32[]{:S(2)}) copy-start(bf16[80,5120]{1,0:T(8,128)(2,1)} %copy-done.7) | copy-start | bytes 2457604 | tf_op jit(solution)/shard_map/while
  216.0 9.9 %copy-start.10 = (bf16[80,5120]{1,0:T(8,128)(2,1)S(1)}, bf16[80,5120]{1,0:T(8,128)(2,1)}, u32[]{:S(2)}) copy-start(bf16[80,5120]{1,0:T(8,128)(2,1)} %copy-done.9) | copy-start | bytes 2457604 | tf_op jit(solution)/shard_map/while
  216.0 9.9 %copy-start.20 = (bf16[80,2560]{1,0:T(8,128)(2,1)S(1)}, bf16[80,2560]{1,0:T(8,128)(2,1)}, u32[]{:S(2)}) copy-start(bf16[80,2560]{1,0:T(8,128)(2,1)} %copy-done.19) | copy-start | bytes 1228804 | tf_op jit(solution)/shard_map/while
  216.0 9.9 %copy-start.22 = (bf16[80,2560]{1,0:T(8,128)(2,1)S(1)}, bf16[80,2560]{1,0:T(8,128)(2,1)}, u32[]{:S(2)}) copy-start(bf16[80,2560]{1,0:T(8,128)(2,1)} %copy-done.21) | copy-start | bytes 1228804 | tf_op jit(solution)/shard_map/while
  226.0 15.2 %copy-start.19 = (bf16[80,2560]{1,0:T(8,128)(2,1)}, bf16[80,2560]{1,0:T(8,128)(2,1)S(1)}, u32[]{:S(2)}) copy-start(bf16[80,2560]{1,0:T(8,128)(2,1)S(1)} %get-tuple-element.738) | copy-start | bytes 1228804 | tf_op jit(solution)/shard_map/while
  226.0 15.2 %copy-start.21 = (bf16[80,2560]{1,0:T(8,128)(2,1)}, bf16[80,2560]{1,0:T(8,128)(2,1)S(1)}, u32[]{:S(2)}) copy-start(bf16[80,2560]{1,0:T(8,128)(2,1)S(1)} %get-tuple-element.736) | copy-start | bytes 1228804 | tf_op jit(solution)/shard_map/while
  226.0 16.7 %copy-start.7 = (bf16[80,5120]{1,0:T(8,128)(2,1)}, bf16[80,5120]{1,0:T(8,128)(2,1)S(1)}, u32[]{:S(2)}) copy-start(bf16[80,5120]{1,0:T(8,128)(2,1)S(1)} %get-tuple-element.737) | copy-start | bytes 2457604 | tf_op jit(solution)/shard_map/while
  226.0 16.7 %copy-start.9 = (bf16[80,5120]{1,0:T(8,128)(2,1)}, bf16[80,5120]{1,0:T(8,128)(2,1)S(1)}, u32[]{:S(2)}) copy-start(bf16[80,5120]{1,0:T(8,128)(2,1)S(1)} %get-tuple-element.739) | copy-start | bytes 2457604 | tf_op jit(solution)/shard_map/while
  288.1 15.2 %copy-start.19 = (bf16[80,2560]{1,0:T(8,128)(2,1)}, bf16[80,2560]{1,0:T(8,128)(2,1)S(1)}, u32[]{:S(2)}) copy-start(bf16[80,2560]{1,0:T(8,128)(2,1)S(1)} %get-tuple-element.738) | copy-start | bytes 1228804 | tf_op jit(solution)/shard_map/while
  288.2 15.2 %copy-start.21 = (bf16[80,2560]{1,0:T(8,128)(2,1)}, bf16[80,2560]{1,0:T(8,128)(2,1)S(1)}, u32[]{:S(2)}) copy-start(bf16[80,2560]{1,0:T(8,128)(2,1)S(1)} %get-tuple-element.736) | copy-start | bytes 1228804 | tf_op jit(solution)/shard_map/while
  288.2 16.7 %copy-start.7 = (bf16[80,5120]{1,0:T(8,128)(2,1)}, bf16[80,5120]{1,0:T(8,128)(2,1)S(1)}, u32[]{:S(2)}) copy-start(bf16[80,5120]{1,0:T(8,128)(2,1)S(1)} %get-tuple-element.737) | copy-start | bytes 2457604 | tf_op jit(solution)/shard_map/while
  288.2 16.7 %copy-start.9 = (bf16[80,5120]{1,0:T(8,128)(2,1)}, bf16[80,5120]{1,0:T(8,128)(2,1)S(1)}, u32[]{:S(2)}) copy-start(bf16[80,5120]{1,0:T(8,128)(2,1)S(1)} %get-tuple-element.739) | copy-start | bytes 2457604 | tf_op jit(solution)/shard_map/while
  340.5 9.9 %copy-start.22 = (bf16[80,2560]{1,0:T(8,128)(2,1)S(1)}, bf16[80,2560]{1,0:T(8,128)(2,1)}, u32[]{:S(2)}) copy-start(bf16[80,2560]{1,0:T(8,128)(2,1)} %copy-done.21) | copy-start | bytes 1228804 | tf_op jit(solution)/shard_map/while
  350.5 223.0 %copy-start.45 = (u32[256]{0:T(256)S(1)}, u32[256]{0:T(256)}, u32[]{:S(2)}) copy-start(u32[256]{0:T(256)} %constant.104) | copy-start | bytes 3076
  350.5 224.2 %copy-start.31 = (bf16[80,128]{1,0:T(8,128)(2,1)S(1)}, bf16[80,128]{1,0:T(8,128)(2,1)}, u32[]{:S(2)}) copy-start(bf16[80,128]{1,0:T(8,128)(2,1)} %copy-done.30) | copy-start | bytes 61444
  350.5 224.2 %copy-start.33 = (bf16[80,128]{1,0:T(8,128)(2,1)S(1)}, bf16[80,128]{1,0:T(8,128)(2,1)}, u32[]{:S(2)}) copy-start(bf16[80,128]{1,0:T(8,128)(2,1)} %copy-done.32) | copy-start | bytes 61444
  350.5 224.2 %copy-start.43 = (f32[80]{0:T(128)S(1)}, f32[80]{0:T(128)}, u32[]{:S(2)}) copy-start(f32[80]{0:T(128)} %copy-done.42) | copy-start | bytes 964
  350.5 306.2 %all-reduce.6.cloned.1.call-start = ((), (), s32[]{:S(2)}) async-start(), calls=%async_computation.2 | async-start | bytes 1638400
  (60 other events, 228.9 us)
Sparse Core Ops, SparseCore 0:
  350.6 221.8 reduce-scatter.1
  575.2 81.5 all-reduce.5
where the time goes:
time: 674 us; the launch traced here: 666 us
  waiting for transfers between devices  226 us (34%)
  local copies, waits for them, and re-layouts  96 us (14%)
  other arithmetic  93.6 us (14%)
  matrix products  93.3 us (14%)
  blocking collectives  75 us (11%)
  loops' own time  65.5 us (10%)
  between operations  16.1 us (2%)
    reduce_scatter x1, waiting for transfers between devices, on_device(): lax.psum_scatter(fold_rows().astype(jnp.bfloat16), 'arc', scatter_dimensi...  220 us
    unnamed x1, blocking collectives  75 us
    another operation x1, loops' own time, fold_rows(): lax.map(one_block, jnp.arange(lax.axis_size('arc') * (half_width // membe...  65.2 us
    while x156, local copies, waits for them, and re-layouts  63.3 us
    dot_general x40, matrix products, above_only(): lax.dot_general(above_cols, above_tile, contract_dims, preferred_element_...  44.9 us
    dynamic_update_slice x4, other arithmetic, fold_rows(): lax.map(one_block, jnp.arange(lax.axis_size('arc') * (half_width // membe...  39.3 us
    dot_general x20, matrix products, mirror_only(): lax.dot_general(mirror_cols, mirror_tile, contract_dims, preferred_elemen...  28.7 us
    another operation x6, other arithmetic, local_system(): factor = jnp.linalg.cholesky(normal_ll)  24.8 us
  transfers between devices with their start and end apart: 2, of which 2 were waited for; matrix products, arithmetic and copies ran while one was open for 1% of the time, Pallas kernels for 0%

commit v1 on v0

v1 whole, which is shorter than its diff:
```python
import jax
import jax.numpy as jnp
from jax import lax
from jax.experimental import pallas as pl
from jax.experimental.pallas import tpu as pltpu
from jax.sharding import PartitionSpec as P

NX = 4
NY = 4
NZ = 8
OBS = 80
WIDTH = 5120
CHUNK = 640
NCHUNK = 8
ROWS = 320
UNIT = 416
ZUNIT = 112
F32 = jnp.float32
BF16 = jnp.bfloat16
MESH = pl.DeviceIdType.MESH


def split(v):
    hi = v.astype(BF16)
    lo = (v - hi.astype(F32)).astype(BF16)
    return hi, lo


def iota(shape, dim):
    return lax.broadcasted_iota(jnp.int32, shape, dim)


def dot(a, b):
    return jnp.dot(a, b, preferred_element_type=F32)


def dot_t(a, b):
    return lax.dot_general(a, b, (((1,), (1,)), ((), ())), preferred_element_type=F32)


def kernel(
    ns_ref,
    kw_ref,
    mw_ref,
    design_ref,
    nuis_ref,
    obs_ref,
    arc_ref,
    kind_ref,
    out_ref,
    small_ref,
    dall,
    aall,
    vsend,
    vall,
    ahi,
    alo,
    tt,
    bout,
    rrel,
    rdir,
    rsum,
    fz,
    zf,
    zs,
    zr,
    of,
    ld_sem,
    xs_p,
    xs_m,
    xf_p,
    xf_m,
    xr,
    ps,
    pr,
    as_sem,
    ar,
    aps,
    apr,
    vs_sem,
    vr,
    ys1,
    ys2,
    ys3,
    yr1,
    yr2,
    yr3,
    zs_sem,
    zr_sem,
):
    mission = lax.axis_index("mission")
    arc = lax.axis_index("arc")
    x = mission // 2
    zl = mission % 2
    zh = arc // 8
    y = (arc // 2) % 4
    core = arc % 2
    s = 4 * zl + zh
    other = 1 - core

    def dev(dx, dy, ds, dc):
        return (2 * dx + ds // 4, 8 * (ds % 4) + 2 * dy + dc)

    xp = (x + 1) % 4
    xm = (x + 3) % 4
    x2 = (x + 2) % 4
    yp = (y + 1) % 4
    ym = (y + 3) % 4

    def block(b):
        return pl.ds(pl.multiple_of(b * OBS, OBS), OBS)

    def load(c):
        return pltpu.make_async_copy(
            design_ref.at[:, pl.ds(c * CHUNK, CHUNK)],
            dall.at[c, block(core), :],
            ld_sem.at[c],
        )

    for c in range(NCHUNK):
        load(c).start()

    barrier = pltpu.get_barrier_semaphore()
    peers = [dev(xp, y, s, core), dev(xm, y, s, core), dev(x2, y, s, core)]
    peers += [dev(xp, y, s, other), dev(xm, y, s, other), dev(x2, y, s, other)]
    peers += [dev(x, y, s, other), dev(x, yp, s, core), dev(x, ym, s, core)]
    for d in range(1, NZ):
        peers.append(dev(x, y, (s + d) % NZ, core))
    for peer in peers:
        pl.semaphore_signal(barrier, inc=1, device_id=peer, device_id_type=MESH)
    pl.semaphore_wait(barrier, len(peers))

    def remote(src, dst, ssem, rsem, to):
        return pltpu.make_async_remote_copy(
            src_ref=src, dst_ref=dst, send_sem=ssem, recv_sem=rsem, device_id=to, device_id_type=MESH
        )

    def own_p(c):
        return remote(
            dall.at[c, block(core), :],
            dall.at[c, block(2 + core), :],
            xs_p.at[c],
            xr.at[0, c],
            dev(xp, y, s, core),
        )

    def own_m(c):
        return remote(
            dall.at[c, block(core), :],
            dall.at[c, block(4 + core), :],
            xs_m.at[c],
            xr.at[1, c],
            dev(xm, y, s, core),
        )

    def fwd_p(p):
        return remote(
            dall.at[p, block(2 + core), :],
            dall.at[p, block(6 + core), :],
            xf_p.at[p],
            xr.at[2, p],
            dev(xp, y, s, core),
        )

    def fwd_m(p):
        c = 7 - p
        return remote(
            dall.at[c, block(4 + core), :],
            dall.at[c, block(6 + core), :],
            xf_m.at[p],
            xr.at[2, c],
            dev(xm, y, s, core),
        )

    def recv_x(slot, c):
        ref = dall.at[c, block(2 * slot + core), :]
        return remote(ref, ref, xs_p.at[c], xr.at[slot - 1, c], dev(xp, y, s, core))

    def partner(slot, c):
        ref = dall.at[c, block(2 * slot + core), :]
        return remote(ref, ref, ps.at[slot, c], pr.at[slot, c], dev(x, y, s, other))

    def recv_partner(slot, c):
        ref = dall.at[c, block(2 * slot + other), :]
        return remote(ref, ref, ps.at[slot, c], pr.at[slot, c], dev(x, y, s, other))

    def pair(e, mine):
        if e == 0:
            return mine
        return (e - 1) + (e - 1 >= mine).astype(jnp.int32)

    for c in range(NCHUNK):
        load(c).wait()

    own_p(xp).start()
    own_m(7 - xm).start()
    own_p(7 - xp).start()
    own_m(xm).start()
    own_p(x2).start()
    own_m(7 - x2).start()

    for e in range(4):
        p = pair(e, x)
        partner(0, p).start()
        partner(0, 7 - p).start()

    def own_rest(e):
        pp = pair(e, xp)
        pm = pair(e, xm)

        @pl.when(pp != x2)
        def _():
            own_p(pp).start()

        own_m(pm).start()
        own_p(7 - pp).start()

        @pl.when(pm != x2)
        def _():
            own_m(7 - pm).start()

    own_rest(1)

    lane = iota((OBS, 128), 1)
    sub = iota((OBS, 128), 0)
    eye = lane == sub
    arc_row = jnp.concatenate([arc_ref[...], jnp.full((1, 48), 2, jnp.int32)], axis=1).astype(F32)
    kind_row = jnp.concatenate([kind_ref[...], jnp.zeros((1, 48), jnp.int32)], axis=1)
    obs_row = jnp.concatenate([obs_ref[...], jnp.zeros((1, 48), F32)], axis=1)
    w_row = jnp.zeros((1, 128), F32)
    for k in range(8):
        w_row = jnp.where(kind_row == k, kw_ref[k], w_row)

    def to_col(row):
        return jnp.sum(jnp.where(eye, jnp.broadcast_to(row, (OBS, 128)), 0.0), axis=1, keepdims=True)

    arc_col = to_col(arc_row)
    obs_col = to_col(obs_row)
    size_col = jnp.where(arc_col == 0.0, ns_ref[0], ns_ref[1])
    nuis = jnp.where(lane < size_col, nuis_ref[...].astype(F32), 0.0)
    nuis = jnp.concatenate([nuis, jnp.zeros((48, 128), F32)], axis=0).astype(BF16)
    gram = dot_t(nuis, nuis)[:OBS]
    h = jnp.where(arc_col == arc_row, gram, 0.0) + jnp.where(eye, 1.0 / w_row, 0.0)

    def eliminate(k, h):
        on_col = lane == k
        col = jnp.sum(jnp.where(on_col, h, 0.0), axis=1, keepdims=True)
        row = jnp.sum(jnp.where(sub == k, h, 0.0), axis=0, keepdims=True)
        at = lane[:1] == k
        pivot = jnp.sum(jnp.where(at, row, 0.0), axis=1, keepdims=True)
        row = jnp.where(at, 1.0, row) * (1.0 / pivot)
        return jnp.where(sub == k, row, jnp.where(on_col, 0.0, h) - col * row)

    a = lax.fori_loop(0, OBS, eliminate, h) * mw_ref[0]
    own_b = pl.ds(pl.multiple_of(core * OBS, OBS), OBS)
    aall[own_b, :] = a

    def send_a(slot, to, src_slot, k):
        return remote(
            aall.at[block(2 * src_slot + core), :],
            aall.at[block(2 * slot + core), :],
            as_sem.at[k],
            ar.at[slot - 1],
            to,
        )

    send_a(1, dev(xp, y, s, core), 0, 0).start()
    send_a(2, dev(xm, y, s, core), 0, 1).start()

    def partner_a(slot):
        ref = aall.at[block(2 * slot + core), :]
        return remote(ref, ref, aps.at[slot], apr.at[slot], dev(x, y, s, other))

    def recv_partner_a(slot):
        ref = aall.at[block(2 * slot + other), :]
        return remote(ref, ref, aps.at[slot], apr.at[slot], dev(x, y, s, other))

    partner_a(0).start()

    recv_x(1, xp).wait_recv()
    fwd_p(xp).start()
    recv_x(2, 7 - xm).wait_recv()
    fwd_m(xm).start()
    own_rest(2)
    own_rest(3)
    send_a(1, dev(xp, y, s, core), 0, 0).wait_recv()
    send_a(3, dev(xp, y, s, core), 1, 2).start()
    partner_a(1).start()
    send_a(2, dev(xm, y, s, core), 0, 1).wait_recv()
    partner_a(2).start()

    z_row = jnp.sum(a * obs_col, axis=0, keepdims=True)
    z_hi, z_lo = split(z_row)
    z_two = jnp.concatenate([z_hi.astype(F32), z_lo.astype(F32), jnp.zeros((14, 128), F32)], axis=0)
    z_two = z_two[:, :OBS].astype(BF16)
    a_hi, a_lo = split(a[:, :OBS])
    for c in range(NCHUNK):
        mine = dall[c, own_b, :]
        res = dot(z_two, mine)
        res = res[0:1] + res[1:2]
        for t in range(5):
            tile = 5 * c + t
            vsend[tile // 10, pl.ds(tile % 10, 1), :] = res[:, 128 * t : 128 * t + 128]
        if c >= 4:
            red = dot(a_hi, mine) + dot(a_lo, mine)
            tail = jnp.sum(mine.astype(F32) * red, axis=0, keepdims=True)
            for t in range(5):
                vsend[c - 4, pl.ds(10 + t, 1), :] = tail[:, 128 * t : 128 * t + 128]
    for k in range(4):
        vsend[k, pl.ds(15, 1), :] = jnp.zeros((1, 128), F32)

    v_to = [(x, other), (xp, core), (xp, other), (xm, core), (xm, other), (x2, core), (x2, other)]

    def send_v(k):
        dx, dc = v_to[k]
        return remote(vsend.at[dx], vall.at[k], vs_sem.at[k], vr.at[k], dev(dx, y, s, dc))

    for k in range(7):
        send_v(k).start()

    for slot in (1, 2, 3):
        for c in (x, 7 - x):
            recv_x(slot, c).wait_recv()
            partner(slot, c).start()
    send_a(3, dev(xp, y, s, core), 1, 2).wait_recv()
    partner_a(3).start()
    for k in range(4):
        recv_partner_a(k).wait_recv()

    for b in range(8):
        sel = (iota((128, CHUNK), 1) - OBS * b == iota((128, CHUNK), 0)).astype(F32).astype(BF16)
        hi, lo = split(aall[b * OBS : (b + 1) * OBS, :])
        ahi[b * OBS : (b + 1) * OBS, :] = dot(hi, sel).astype(BF16)
        alo[b * OBS : (b + 1) * OBS, :] = dot(lo, sel).astype(BF16)

    prow = iota((ROWS, CHUNK), 0)
    pcol = iota((ROWS, CHUNK), 1)
    pj = prow >> 3
    py = (pj >= 10).astype(jnp.int32) + (pj >= 20).astype(jnp.int32) + (pj >= 30).astype(jnp.int32)
    target = 80 * (prow & 7) + 20 * py + 10 * core + (pj - 10 * py)

    for slot in range(4):
        recv_partner(slot, x).wait_recv()
        recv_partner(slot, 7 - x).wait_recv()

    for half in range(2):
        hit = (pcol == target) if half == 0 else ((CHUNK - 1 - pcol) == target)
        pick = jnp.where(hit, 1.0, 0.0).astype(BF16)
        chosen = dot_t(pick, dall[x if half == 0 else 7 - x]).astype(BF16)
        tt[half] = (dot(chosen, ahi[...]) + dot(chosen, alo[...])).astype(BF16)

    for k in range(7):
        send_v(k).wait_recv()
    vsum = vsend[x]
    for k in range(7):
        vsum = vsum + vall[k]
    row32 = iota((32, 128), 0)
    lane32 = iota((32, 128), 1)
    spread = jnp.zeros((32, 128), F32)
    for rho in range(15):
        if rho < 10:
            start = 160 * (row32 & 7) + 40 * (row32 >> 3) + 20 * core
            width, at, off = 20, 128 * rho, 0
        else:
            start = 80 * (row32 & 7) + 20 * (row32 >> 3) + 10 * core
            width, at, off = 10, 128 * (rho - 10), 20
        idx = lane32 + at
        keep = (idx >= start) & (idx < start + width)
        vals = jnp.where(keep, jnp.broadcast_to(vsum[rho : rho + 1], (32, 128)), 0.0)
        src = iota((128, 128), 0) + at
        place = iota((128, 128), 1) - off
        quot = (src * (3277 if width == 20 else 6554)) >> 16
        q = jnp.where(src - width * quot == place, 1.0, 0.0).astype(BF16)
        hi, lo = split(vals)
        spread = spread + dot(hi, q) + dot(lo, q)
    for yy in range(4):
        extra = jnp.concatenate([spread[8 * yy : 8 * yy + 8], jnp.zeros((8, 128), F32)], axis=0)
        bout[x, yy, 400:416, :] = extra.astype(BF16)

    def put(q, val):
        for yy in range(4):
            for t in range(5):
                bout[q, yy, 80 * t : 80 * t + 80, :] = val[
                    80 * yy : 80 * yy + 80, 128 * t : 128 * t + 128
                ].astype(BF16)

    rev = jnp.where(iota((128, 128), 0) + iota((128, 128), 1) == 127, 1.0, 0.0).astype(BF16)

    def mirrored(c):
        whole = dall[c]
        parts = []
        for t in range(5):
            parts.append(dot(whole[:, 128 * (4 - t) : 128 * (4 - t) + 128], rev).astype(BF16))
        return jnp.concatenate(parts, axis=1)

    def outputs(p, e):
        put(7 - p, dot(tt[0], dall[7 - p]))
        if e == 0:
            put(p, jnp.where(pcol >= target, dot(tt[0], dall[p]), dot(tt[1], mirrored(7 - p))))
        else:

            @pl.when(p > x)
            def _():
                put(p, dot(tt[0], dall[p]))

            @pl.when(p < x)
            def _():
                put(p, dot(tt[1], mirrored(7 - p)))

            zero = jnp.zeros((16, 128), BF16)
            for yy in range(4):
                bout[p, yy, 400:416, :] = zero
        for yy in range(4):
            bout[7 - p, yy, 400:416, :] = jnp.zeros((16, 128), BF16)

    def y_way(q, up):
        near, far = (yp, ym) if up else (ym, yp)
        far2 = (y + 2) % 4
        s1 = remote(bout.at[q, far2], rrel.at[q], ys1.at[q], yr1.at[q], dev(x, near, s, core))
        s2 = remote(bout.at[q, far], rdir.at[q], ys2.at[q], yr2.at[q], dev(x, far, s, core))
        s3 = remote(bout.at[q, near], rsum.at[q], ys3.at[q], yr3.at[q], dev(x, near, s, core))
        return near, s1, s2, s3

    def y_send(p):
        for q, up in ((p, True), (7 - p, False)):
            near, s1, s2, s3 = y_way(q, up)
            s1.start()
            s2.start()

    def y_relay(p):
        for q, up in ((p, True), (7 - p, False)):
            near, s1, s2, s3 = y_way(q, up)
            s1.wait_recv()
            bout[q, near] = (bout[q, near].astype(F32) + rrel[q].astype(F32)).astype(BF16)
            s3.start()

    def z_copy(p, d):
        to = (s + d) % NZ
        return remote(zs.at[p, to], zr.at[p, s], zs_sem.at[p, to], zr_sem.at[p, s], dev(x, y, to, core))

    def z_recv(p, d):
        frm = (s + d) % NZ
        return remote(zs.at[p, frm], zr.at[p, frm], zs_sem.at[p, frm], zr_sem.at[p, frm], dev(x, y, frm, core))

    zf[...] = jnp.zeros(zf.shape, F32)

    def y_final(p):
        for half, (q, up) in enumerate(((p, True), (7 - p, False))):
            near, s1, s2, s3 = y_way(q, up)
            s2.wait_recv()
            s3.wait_recv()
            fz[half] = bout[q, y].astype(F32) + rdir[q].astype(F32) + rsum[q].astype(F32)
        for k in range(NZ):
            zf[k, 0:50, :] = fz[0, pl.ds(k, 50, stride=8), :]
            zf[k, 50:100, :] = fz[1, pl.ds(k, 50, stride=8), :]
            zf[k, 100:101, :] = fz[0, 400 + k : 401 + k, :]
            zs[p, k] = zf[k].astype(BF16)
        for d in range(1, NZ):
            z_copy(p, d).start()

    def z_final(p, e):
        total = zs[p, s].astype(F32)
        for d in range(1, NZ):
            z_recv(p, d).wait_recv()
            total = total + zr[p, (s + d) % NZ].astype(F32)
        of[...] = total
        for half, q in enumerate((p, 7 - p)):
            for t in range(5):
                at = pl.ds(pl.multiple_of(q * CHUNK + 128 * t, 128), 128)
                out_ref[:, at] = of[50 * half + 10 * t : 50 * half + 10 * t + 10, :]
        if e == 0:
            small_ref[...] = of[100:101, :]

    def relays(e):
        pp = pair(e, xp)
        pm = pair(e, xm)

        @pl.when(pp != x)
        def _():
            recv_x(1, pp).wait_recv()

        fwd_p(pp).start()

        @pl.when(pm != x)
        def _():
            recv_x(2, 7 - pm).wait_recv()

        fwd_m(pm).start()

    def line(e):
        p = pair(e, x)
        for slot in (1, 2, 3):
            for c, upper in ((p, False), (7 - p, True)):
                if slot == 3 or (slot == 1) == upper:
                    recv_x(slot, c).wait_recv()
                partner(slot, c).start()
        for slot in range(4):
            recv_partner(slot, p).wait_recv()
            recv_partner(slot, 7 - p).wait_recv()

    order = [pair(e, x) for e in range(4)]
    outputs(order[0], 0)
    y_send(order[0])
    for e in range(1, 4):
        relays(e)
    line(1)
    y_relay(order[0])
    outputs(order[1], 1)
    y_send(order[1])
    line(2)
    outputs(order[2], 2)
    y_send(order[2])
    y_relay(order[1])
    y_final(order[0])
    line(3)
    outputs(order[3], 3)
    y_send(order[3])
    y_relay(order[2])
    y_final(order[1])
    y_relay(order[3])
    z_final(order[0], 0)
    y_final(order[2])
    z_final(order[1], 1)
    y_final(order[3])
    z_final(order[2], 2)
    z_final(order[3], 3)

    for c in range(NCHUNK):
        own_p(c).wait_send()
        own_m(c).wait_send()
    for p in range(4):
        fwd_p(p).wait_send()
        fwd_m(p).wait_send()
        partner_a(p).wait_send()
        for c in range(NCHUNK):
            partner(p, c).wait_send()
    send_a(1, dev(xp, y, s, core), 0, 0).wait_send()
    send_a(2, dev(xm, y, s, core), 0, 1).wait_send()
    send_a(3, dev(xp, y, s, core), 1, 2).wait_send()
    for k in range(7):
        send_v(k).wait_send()
    for q in range(NCHUNK):
        near, s1, s2, s3 = y_way(q, q < 4)
        s1.wait_send()
        s2.wait_send()
        s3.wait_send()
    for p in range(4):
        for d in range(1, NZ):
            z_copy(p, d).wait_send()


def on_device(design, nuisance, observed, arc_of_row, nuis_size, kinds, kind_weight, mission_weight):
    vmem = pl.BlockSpec(memory_space=pltpu.VMEM)
    smem = pl.BlockSpec(memory_space=pltpu.SMEM)
    dma = pltpu.SemaphoreType.DMA
    scratch = [
        pltpu.VMEM((NCHUNK, 640, CHUNK), BF16),
        pltpu.VMEM((640, 128), F32),
        pltpu.VMEM((4, 16, 128), F32),
        pltpu.VMEM((7, 16, 128), F32),
        pltpu.VMEM((640, 640), BF16),
        pltpu.VMEM((640, 640), BF16),
        pltpu.VMEM((2, ROWS, 640), BF16),
        pltpu.VMEM((NCHUNK, 4, UNIT, 128), BF16),
        pltpu.VMEM((NCHUNK, UNIT, 128), BF16),
        pltpu.VMEM((NCHUNK, UNIT, 128), BF16),
        pltpu.VMEM((NCHUNK, UNIT, 128), BF16),
        pltpu.VMEM((2, UNIT, 128), F32),
        pltpu.VMEM((NZ, ZUNIT, 128), F32),
        pltpu.VMEM((4, NZ, ZUNIT, 128), BF16),
        pltpu.VMEM((4, NZ, ZUNIT, 128), BF16),
        pltpu.VMEM((ZUNIT, 128), F32),
        dma((8,)),
        dma((8,)),
        dma((8,)),
        dma((4,)),
        dma((4,)),
        dma((3, 8)),
        dma((4, 8)),
        dma((4, 8)),
        dma((3,)),
        dma((3,)),
        dma((4,)),
        dma((4,)),
        dma((7,)),
        dma((7,)),
        dma((8,)),
        dma((8,)),
        dma((8,)),
        dma((8,)),
        dma((8,)),
        dma((8,)),
        dma((4, 8)),
        dma((4, 8)),
    ]
    fold, small = pl.pallas_call(
        kernel,
        out_shape=(
            jax.ShapeDtypeStruct((10, WIDTH), F32),
            jax.ShapeDtypeStruct((1, 128), F32),
        ),
        in_specs=[smem, smem, smem, pl.BlockSpec(memory_space=pl.ANY), vmem, vmem, vmem, vmem],
        out_specs=(vmem, vmem),
        scratch_shapes=scratch,
        compiler_params=pltpu.CompilerParams(
            collective_id=0, has_side_effects=True, vmem_limit_bytes=56 * 1024 * 1024
        ),
    )(
        nuis_size,
        kind_weight,
        mission_weight,
        design,
        nuisance,
        observed[None, :],
        arc_of_row[None, :],
        kinds[None, :],
    )
    return (fold, small[0, :20], small[0, 20:30])


def solution(mesh):
    rows = P(("mission", "arc"))
    wide = P(("mission", "arc"), None)
    return jax.shard_map(
        on_device,
        mesh=mesh,
        in_specs=(wide, wide, rows, rows, rows, rows, P(), P("mission")),
        out_specs=(wide, rows, rows),
        check_vma=False,
    )
```

time: 674 us -> 89.2 us (0.13); the launches traced: 666 us -> 87.9 us
  waiting for transfers between devices: 226 us -> 0 us
  other arithmetic: 93.6 us -> 0 us
  matrix products: 93.3 us -> 0 us
  local copies, waits for them, and re-layouts: 96 us -> 3.41 us
  Pallas kernels: 0 us -> 83.2 us
  blocking collectives: 75 us -> 0 us
  loops' own time: 65.5 us -> 0 us
  between operations: 16.1 us -> 1.3 us
    reduce_scatter x1 -> x0, waiting for transfers between devices: 220 us -> none  [on_device(): lax.psum_scatter(fold_rows().astype(jnp.bfloat16), 'arc', scatter_dimensi...]
    pallas_call x0 -> x1, Pallas kernels: none -> 83.2 us  [on_device(): pl.pallas_call(kernel, out_shape=(jax.ShapeDtypeStruct((10, WIDTH), F32),...]
    dot_general x68 -> x0, matrix products: 81.3 us -> none  [the longest x40 44.9 us: above_only(): lax.dot_general(above_cols, above_tile, contract_dims, preferred_element_...]
    unnamed x1 -> x0, blocking collectives: 75 us -> none
    another operation x41 -> x0, loops' own time: 65.5 us -> none  [the longest x1 65.2 us: fold_rows(): lax.map(one_block, jnp.arange(lax.axis_size('arc') * (half_width // membe...]
    while x156 -> x0, local copies, waits for them, and re-layouts: 63.3 us -> none
    another operation x10 -> x0, other arithmetic: 45.9 us -> none  [the longest x6 24.8 us: local_system(): factor = jnp.linalg.cholesky(normal_ll)]
    dynamic_update_slice x4 -> x0, other arithmetic: 39.3 us -> none  [fold_rows(): lax.map(one_block, jnp.arange(lax.axis_size('arc') * (half_width // membe...]
  transfers between devices with their start and end apart: 2 -> 0, of which waited for: 2 -> 0; matrix products, arithmetic and copies ran while one was open for 1% -> 0% of each run, Pallas kernels for 0% -> 0%
where the time goes in v1:
time: 89.2 us; the launch traced here: 87.9 us
  Pallas kernels  83.2 us (93%)
  local copies, waits for them, and re-layouts  3.41 us (4%)
  between operations  1.3 us (1%)
    pallas_call x1, Pallas kernels, on_device(): pl.pallas_call(kernel, out_shape=(jax.ShapeDtypeStruct((10, WIDTH), F32),...  83.2 us
    unnamed x3, local copies, waits for them, and re-layouts  2.32 us

profile of v1, /device:TPU:6, one launch (start us, length us, event | category | flops | bytes accessed | tf_op | source)
XLA Modules:
  0.0 87.9 jit_solution(10479568540500497788)
XLA Ops:
  1.3 83.2 %shard_map.103 = (f32[10,5120]{1,0:T(8,128)}, f32[1,128]{1,0:T(1,128)}) custom-call(s32[2]{0:T(128)} %ns_ref.1, f32[8]{0:T(128)} %kw_ref.1, f32[1]{0:T(128)S(6)} %copy.12.mw_ref, bf16[80,5120]{1,0:T(8,128)(2,1)} %design_ref.1, bf16[80,128]{1,0:T(8,128)(2,1)} %nuis_ref.1, f32[1,80]{1,0:T(1,128)} %bitcast.7, s32[1,80]{1,0:T(1,128)} %bitcast.8, s32[1,80]{1,0:T(1,128)} %bitcast.9), custom_call_target="tpu_custom_call" | custom-call | tf_op jit(solution)/shard_map/pallas_call | solution.py:596
  84.4 0.0 copy-start
  84.5 0.6 copy-done
  85.1 0.6 slice_bitcast_fusion
  85.6 0.5 slice_bitcast_fusion.1
  86.1 1.7 %copy.13 = f32[10,5120]{1,0:T(8,128)} copy(f32[10,5120]{1,0:T(8,128)} %get-tuple-element.10) | data formatting | bytes 409600
Async XLA Ops:
  84.4 0.6 copy-start

commit v2 on v1

--- a/solution.py
+++ b/solution.py
@@ -43,12 +43,18 @@
     kw_ref,
     mw_ref,
     design_ref,
+    nuis_in,
+    obs_in,
+    arc_in,
+    kind_in,
+    out_ref,
+    right_ref,
+    tail_ref,
     nuis_ref,
     obs_ref,
     arc_ref,
     kind_ref,
-    out_ref,
-    small_ref,
+    in_sem,
     dall,
     aall,
     vsend,
@@ -117,8 +123,16 @@
             ld_sem.at[c],
         )
 
+    small_loads = [
+        pltpu.make_async_copy(src, dst, in_sem.at[k])
+        for k, (src, dst) in enumerate(
+            ((nuis_in, nuis_ref), (obs_in, obs_ref), (arc_in, arc_ref), (kind_in, kind_ref))
+        )
+    ]
     for c in range(NCHUNK):
         load(c).start()
+    for copy in small_loads:
+        copy.start()
 
     barrier = pltpu.get_barrier_semaphore()
     peers = [dev(xp, y, s, core), dev(xm, y, s, core), dev(x2, y, s, core)]
@@ -204,7 +218,7 @@
         partner(0, p).start()
         partner(0, 7 - p).start()
 
-    def own_rest(e):
+    def own_lower(e):
         pp = pair(e, xp)
         pm = pair(e, xm)
 
@@ -213,13 +227,18 @@
             own_p(pp).start()
 
         own_m(pm).start()
+
+    def own_upper(e):
+        pp = pair(e, xp)
+        pm = pair(e, xm)
         own_p(7 - pp).start()
 
         @pl.when(pm != x2)
         def _():
             own_m(7 - pm).start()
 
-    own_rest(1)
+    for copy in small_loads:
+        copy.wait()
 
     lane = iota((OBS, 128), 1)
     sub = iota((OBS, 128), 0)
@@ -242,30 +261,45 @@
     gram = dot_t(nuis, nuis)[:OBS]
     h = jnp.where(arc_col == arc_row, gram, 0.0) + jnp.where(eye, 1.0 / w_row, 0.0)
 
-    def eliminate(k, h):
-        on_col = lane == k
-        col = jnp.sum(jnp.where(on_col, h, 0.0), axis=1, keepdims=True)
-        row = jnp.sum(jnp.where(sub == k, h, 0.0), axis=0, keepdims=True)
-        at = lane[:1] == k
-        pivot = jnp.sum(jnp.where(at, row, 0.0), axis=1, keepdims=True)
-        row = jnp.where(at, 1.0, row) * (1.0 / pivot)
-        return jnp.where(sub == k, row, jnp.where(on_col, 0.0, h) - col * row)
-
-    a = lax.fori_loop(0, OBS, eliminate, h) * mw_ref[0]
+    def eliminate(step, h):
+        k = 2 * step
+        on1 = lane == k
+        on2 = lane == k + 1
+        at1 = on1[:1]
+        at2 = on2[:1]
+        is1 = sub == k
+        is2 = sub == k + 1
+        col1 = jnp.sum(jnp.where(on1, h, 0.0), axis=1, keepdims=True)
+        col2 = jnp.sum(jnp.where(on2, h, 0.0), axis=1, keepdims=True)
+        row1 = jnp.sum(jnp.where(is1, h, 0.0), axis=0, keepdims=True)
+        row2 = jnp.sum(jnp.where(is2, h, 0.0), axis=0, keepdims=True)
+        p11 = jnp.sum(jnp.where(at1, row1, 0.0), axis=1, keepdims=True)
+        p12 = jnp.sum(jnp.where(at2, row1, 0.0), axis=1, keepdims=True)
+        p22 = jnp.sum(jnp.where(at2, row2, 0.0), axis=1, keepdims=True)
+        inv = 1.0 / (p11 * p22 - p12 * p12)
+        row1 = jnp.where(at1, 1.0, jnp.where(at2, 0.0, row1))
+        row2 = jnp.where(at2, 1.0, jnp.where(at1, 0.0, row2))
+        new1 = (p22 * inv) * row1 - (p12 * inv) * row2
+        new2 = (p11 * inv) * row2 - (p12 * inv) * row1
+        rest = jnp.where(on1 | on2, 0.0, h) - col1 * new1 - col2 * new2
+        return jnp.where(is1, new1, jnp.where(is2, new2, rest))
+
+    a = lax.fori_loop(0, OBS // 2, eliminate, h) * mw_ref[0]
     own_b = pl.ds(pl.multiple_of(core * OBS, OBS), OBS)
     aall[own_b, :] = a
 
-    def send_a(slot, to, src_slot, k):
+    def send_a(slot):
+        to = {1: xp, 2: xm, 3: x2}[slot]
         return remote(
-            aall.at[block(2 * src_slot + core), :],
+            aall.at[own_b, :],
             aall.at[block(2 * slot + core), :],
-            as_sem.at[k],
+            as_sem.at[slot - 1],
             ar.at[slot - 1],
-            to,
-        )
-
-    send_a(1, dev(xp, y, s, core), 0, 0).start()
-    send_a(2, dev(xm, y, s, core), 0, 1).start()
+            dev(to, y, s, core),
+        )
+
+    for slot in (1, 2, 3):
+        send_a(slot).start()
 
     def partner_a(slot):
         ref = aall.at[block(2 * slot + core), :]
@@ -276,18 +310,6 @@
         return remote(ref, ref, aps.at[slot], apr.at[slot], dev(x, y, s, other))
 
     partner_a(0).start()
-
-    recv_x(1, xp).wait_recv()
-    fwd_p(xp).start()
-    recv_x(2, 7 - xm).wait_recv()
-    fwd_m(xm).start()
-    own_rest(2)
-    own_rest(3)
-    send_a(1, dev(xp, y, s, core), 0, 0).wait_recv()
-    send_a(3, dev(xp, y, s, core), 1, 2).start()
-    partner_a(1).start()
-    send_a(2, dev(xm, y, s, core), 0, 1).wait_recv()
-    partner_a(2).start()
 
     z_row = jnp.sum(a * obs_col, axis=0, keepdims=True)
     z_hi, z_lo = split(z_row)
@@ -318,14 +340,28 @@
     for k in range(7):
         send_v(k).start()
 
-    for slot in (1, 2, 3):
+    recv_x(1, xp).wait_recv()
+    fwd_p(xp).start()
+    recv_x(2, 7 - xm).wait_recv()
+    fwd_m(xm).start()
+    own_lower(1)
+    own_upper(1)
+    own_lower(2)
+    own_upper(2)
+    own_lower(3)
+
+    for slot in (1, 2):
         for c in (x, 7 - x):
             recv_x(slot, c).wait_recv()
             partner(slot, c).start()
-    send_a(3, dev(xp, y, s, core), 1, 2).wait_recv()
-    partner_a(3).start()
-    for k in range(4):
-        recv_partner_a(k).wait_recv()
+    for slot in (1, 2, 3):
+        send_a(slot).wait_recv()
+        partner_a(slot).start()
+    for c in (x, 7 - x):
+        recv_x(3, c).wait_recv()
+        partner(3, c).start()
+    for slot in range(4):
+        recv_partner_a(slot).wait_recv()
 
     for b in range(8):
         sel = (iota((128, CHUNK), 1) - OBS * b == iota((128, CHUNK), 0)).astype(F32).astype(BF16)
@@ -338,16 +374,6 @@
     pj = prow >> 3
     py = (pj >= 10).astype(jnp.int32) + (pj >= 20).astype(jnp.int32) + (pj >= 30).astype(jnp.int32)
     target = 80 * (prow & 7) + 20 * py + 10 * core + (pj - 10 * py)
-
-    for slot in range(4):
-        recv_partner(slot, x).wait_recv()
-        recv_partner(slot, 7 - x).wait_recv()
-
-    for half in range(2):
-        hit = (pcol == target) if half == 0 else ((CHUNK - 1 - pcol) == target)
-        pick = jnp.where(hit, 1.0, 0.0).astype(BF16)
-        chosen = dot_t(pick, dall[x if half == 0 else 7 - x]).astype(BF16)
-        tt[half] = (dot(chosen, ahi[...]) + dot(chosen, alo[...])).astype(BF16)
 
     for k in range(7):
         send_v(k).wait_recv()
@@ -377,6 +403,16 @@
         extra = jnp.concatenate([spread[8 * yy : 8 * yy + 8], jnp.zeros((8, 128), F32)], axis=0)
         bout[x, yy, 400:416, :] = extra.astype(BF16)
 
+    for slot in range(4):
+        recv_partner(slot, x).wait_recv()
+        recv_partner(slot, 7 - x).wait_recv()
+
+    for half in range(2):
+        hit = (pcol == target) if half == 0 else ((CHUNK - 1 - pcol) == target)
+        pick = jnp.where(hit, 1.0, 0.0).astype(BF16)
+        chosen = dot_t(pick, dall[x if half == 0 else 7 - x]).astype(BF16)
+        tt[half] = (dot(chosen, ahi[...]) + dot(chosen, alo[...])).astype(BF16)
+
     def put(q, val):
         for yy in range(4):
             for t in range(5):
@@ -393,8 +429,37 @@
             parts.append(dot(whole[:, 128 * (4 - t) : 128 * (4 - t) + 128], rev).astype(BF16))
         return jnp.concatenate(parts, axis=1)
 
+    def y_first(q, up):
+        near = yp if up else ym
+        far2 = (y + 2) % 4
+        return remote(bout.at[q, far2], rrel.at[q], ys1.at[q], yr1.at[q], dev(x, near, s, core))
+
+    def y_back(q, up):
+        far = ym if up else yp
+        return remote(bout.at[q, far], rdir.at[q], ys2.at[q], yr2.at[q], dev(x, far, s, core))
+
+    def y_sum(q, up):
+        near = yp if up else ym
+        return remote(bout.at[q, near], rsum.at[q], ys3.at[q], yr3.at[q], dev(x, near, s, core))
+
+    def y_send(q, up):
+        y_first(q, up).start()
+        y_back(q, up).start()
+
+    def y_relay(p):
+        for q, up in ((7 - p, False), (p, True)):
+            near = yp if up else ym
+            y_first(q, up).wait_recv()
+            bout[q, near] = (bout[q, near].astype(F32) + rrel[q].astype(F32)).astype(BF16)
+            y_sum(q, up).start()
+
+    zero = jnp.zeros((16, 128), BF16)
+
     def outputs(p, e):
+        for yy in range(4):
+            bout[7 - p, yy, 400:416, :] = zero
         put(7 - p, dot(tt[0], dall[7 - p]))
+        y_send(7 - p, False)
         if e == 0:
             put(p, jnp.where(pcol >= target, dot(tt[0], dall[p]), dot(tt[1], mirrored(7 - p))))
         else:
@@ -407,32 +472,9 @@
             def _():
                 put(p, dot(tt[1], mirrored(7 - p)))
 
-            zero = jnp.zeros((16, 128), BF16)
             for yy in range(4):
                 bout[p, yy, 400:416, :] = zero
-        for yy in range(4):
-            bout[7 - p, yy, 400:416, :] = jnp.zeros((16, 128), BF16)
-
-    def y_way(q, up):
-        near, far = (yp, ym) if up else (ym, yp)
-        far2 = (y + 2) % 4
-        s1 = remote(bout.at[q, far2], rrel.at[q], ys1.at[q], yr1.at[q], dev(x, near, s, core))
-        s2 = remote(bout.at[q, far], rdir.at[q], ys2.at[q], yr2.at[q], dev(x, far, s, core))
-        s3 = remote(bout.at[q, near], rsum.at[q], ys3.at[q], yr3.at[q], dev(x, near, s, core))
-        return near, s1, s2, s3
-
-    def y_send(p):
-        for q, up in ((p, True), (7 - p, False)):
-            near, s1, s2, s3 = y_way(q, up)
-            s1.start()
-            s2.start()
-
-    def y_relay(p):
-        for q, up in ((p, True), (7 - p, False)):
-            near, s1, s2, s3 = y_way(q, up)
-            s1.wait_recv()
-            bout[q, near] = (bout[q, near].astype(F32) + rrel[q].astype(F32)).astype(BF16)
-            s3.start()
+        y_send(p, True)
 
     def z_copy(p, d):
         to = (s + d) % NZ
@@ -446,9 +488,8 @@
 
     def y_final(p):
         for half, (q, up) in enumerate(((p, True), (7 - p, False))):
-            near, s1, s2, s3 = y_way(q, up)
-            s2.wait_recv()
-            s3.wait_recv()
+            y_back(q, up).wait_recv()
+            y_sum(q, up).wait_recv()
             fz[half] = bout[q, y].astype(F32) + rdir[q].astype(F32) + rsum[q].astype(F32)
         for k in range(NZ):
             zf[k, 0:50, :] = fz[0, pl.ds(k, 50, stride=8), :]
@@ -469,19 +510,25 @@
                 at = pl.ds(pl.multiple_of(q * CHUNK + 128 * t, 128), 128)
                 out_ref[:, at] = of[50 * half + 10 * t : 50 * half + 10 * t + 10, :]
         if e == 0:
-            small_ref[...] = of[100:101, :]
+            right_ref[...] = of[100:101, 0:20]
+            tail_ref[...] = of[100:101, 20:30]
 
     def relays(e):
         pp = pair(e, xp)
         pm = pair(e, xm)
-
-        @pl.when(pp != x)
+        need_p = pp != x
+        need_m = pm != x
+        if e > 1:
+            need_p = need_p & (pp != pair(1, x))
+            need_m = need_m & (pm != pair(1, x))
+
+        @pl.when(need_p)
         def _():
             recv_x(1, pp).wait_recv()
 
         fwd_p(pp).start()
 
-        @pl.when(pm != x)
+        @pl.when(need_m)
         def _():
             recv_x(2, 7 - pm).wait_recv()
 
@@ -489,6 +536,16 @@
 
     def line(e):
         p = pair(e, x)
+        if e == 1:
+
+            @pl.when((p != xp) & (p != pair(1, xp)))
+            def _():
+                recv_x(1, p).wait_recv()
+
+            @pl.when((p != xm) & (p != pair(1, xm)))
+            def _():
+                recv_x(2, 7 - p).wait_recv()
+
         for slot in (1, 2, 3):
             for c, upper in ((p, False), (7 - p, True)):
                 if slot == 3 or (slot == 1) == upper:
@@ -500,21 +557,19 @@
 
     order = [pair(e, x) for e in range(4)]
     outputs(order[0], 0)
-    y_send(order[0])
-    for e in range(1, 4):
-        relays(e)
+    relays(1)
+    own_upper(3)
     line(1)
+    outputs(order[1], 1)
     y_relay(order[0])
-    outputs(order[1], 1)
-    y_send(order[1])
+    relays(2)
+    relays(3)
     line(2)
     outputs(order[2], 2)
-    y_send(order[2])
     y_relay(order[1])
-    y_final(order[0])
     line(3)
     outputs(order[3], 3)
-    y_send(order[3])
+    y_final(order[0])
     y_relay(order[2])
     y_final(order[1])
     y_relay(order[3])
@@ -534,16 +589,14 @@
         partner_a(p).wait_send()
         for c in range(NCHUNK):
             partner(p, c).wait_send()
-    send_a(1, dev(xp, y, s, core), 0, 0).wait_send()
-    send_a(2, dev(xm, y, s, core), 0, 1).wait_send()
-    send_a(3, dev(xp, y, s, core), 1, 2).wait_send()
+    for slot in (1, 2, 3):
+        send_a(slot).wait_send()
     for k in range(7):
         send_v(k).wait_send()
     for q in range(NCHUNK):
-        near, s1, s2, s3 = y_way(q, q < 4)
-        s1.wait_send()
-        s2.wait_send()
-        s3.wait_send()
+        y_first(q, q < 4).wait_send()
+        y_back(q, q < 4).wait_send()
+        y_sum(q, q < 4).wait_send()
     for p in range(4):
         for d in range(1, NZ):
             z_copy(p, d).wait_send()
@@ -554,6 +607,11 @@
     smem = pl.BlockSpec(memory_space=pltpu.SMEM)
     dma = pltpu.SemaphoreType.DMA
     scratch = [
+        pltpu.VMEM((OBS, 128), BF16),
+        pltpu.VMEM((1, OBS), F32),
+        pltpu.VMEM((1, OBS), jnp.int32),
+        pltpu.VMEM((1, OBS), jnp.int32),
+        dma((4,)),
         pltpu.VMEM((NCHUNK, 640, CHUNK), BF16),
         pltpu.VMEM((640, 128), F32),
         pltpu.VMEM((4, 16, 128), F32),
@@ -593,14 +651,15 @@
         dma((4, 8)),
         dma((4, 8)),
     ]
-    fold, small = pl.pallas_call(
+    fold, right, tail = pl.pallas_call(
         kernel,
         out_shape=(
             jax.ShapeDtypeStruct((10, WIDTH), F32),
-            jax.ShapeDtypeStruct((1, 128), F32),
+            jax.ShapeDtypeStruct((1, 20), F32),
+            jax.ShapeDtypeStruct((1, 10), F32),
         ),
-        in_specs=[smem, smem, smem, pl.BlockSpec(memory_space=pl.ANY), vmem, vmem, vmem, vmem],
-        out_specs=(vmem, vmem),
+        in_specs=[smem] * 3 + [pl.BlockSpec(memory_space=pl.ANY)] * 5,
+        out_specs=(vmem, vmem, vmem),
         scratch_shapes=scratch,
         compiler_params=pltpu.CompilerParams(
             collective_id=0, has_side_effects=True, vmem_limit_bytes=56 * 1024 * 1024
@@ -615,7 +674,7 @@
         arc_of_row[None, :],
         kinds[None, :],
     )
-    return (fold, small[0, :20], small[0, 20:30])
+    return (fold, right[0], tail[0])
 
 
 def solution(mesh):

time: 89.2 us -> 79.9 us (0.90); the launches traced: 87.9 us -> 79.7 us
  Pallas kernels: 83.2 us -> 75.5 us
    pallas_call x1, Pallas kernels: 83.2 us -> 75.5 us  [on_device(): pl.pallas_call(kernel, out_shape=(jax.ShapeDtypeStruct((10, WIDTH), F32),...]
    squeeze x2 -> x0, local copies, waits for them, and re-layouts: 1.09 us -> none  [on_device(): return (fold, small[0, :20], small[0, 20:30])]
    unnamed x3 -> x7, local copies, waits for them, and re-layouts: 2.32 us -> 2.9 us
where the time goes in v2:
time: 79.9 us; the launch traced here: 79.7 us
  Pallas kernels  75.5 us (94%)
  local copies, waits for them, and re-layouts  2.9 us (4%)
  between operations  1.3 us (2%)
    pallas_call x1, Pallas kernels, on_device(): pl.pallas_call(kernel, out_shape=(jax.ShapeDtypeStruct((10, WIDTH), F32),...  75.5 us
    unnamed x7, local copies, waits for them, and re-layouts  2.9 us

profile of v2, /device:TPU:6, one launch (start us, length us, event | category | flops | bytes accessed | tf_op | source)
XLA Modules:
  0.0 79.7 jit_solution(17184844719759101689)
XLA Ops:
  1.3 75.5 %shard_map.103 = (f32[10,5120]{1,0:T(8,128)}, f32[1,20]{1,0:T(1,128)}, f32[1,10]{1,0:T(1,128)}) custom-call(s32[2]{0:T(128)} %ns_ref.1, f32[8]{0:T(128)} %kw_ref.1, f32[1]{0:T(128)S(6)} %copy.14.mw_ref, bf16[80,5120]{1,0:T(8,128)(2,1)} %design_ref.1, bf16[80,128]{1,0:T(8,128)(2,1)} %nuis_in.1, f32[1,80]{1,0:T(1,128)} %bitcast.5, s32[1,80]{1,0:T(1,128)} %bitcast.6, ...), custom_call_target="tpu_custom_call" | custom-call | tf_op jit(solution)/shard_map/pallas_call | solution.py:654
  76.8 0.0 copy-start.1
  76.8 1.7 %copy.15 = f32[10,5120]{1,0:T(8,128)} copy(f32[10,5120]{1,0:T(8,128)} %get-tuple-element.12) | data formatting | bytes 409600
  78.5 0.0 copy-done.1
  78.5 0.0 copy-start
  78.5 0.5 copy.16
  79.1 0.2 copy-done
  79.2 0.5 copy.17
Async XLA Ops:
  76.8 1.7 %copy-start.1 = (f32[1,20]{1,0:T(1,128)S(1)}, f32[1,20]{1,0:T(1,128)}, u32[]{:S(2)}) copy-start(f32[1,20]{1,0:T(1,128)} %get-tuple-element.7) | copy-start | bytes 244
  78.5 0.7 copy-start

commit v3 on v2

--- a/solution.py
+++ b/solution.py
@@ -14,6 +14,7 @@
 NCHUNK = 8
 ROWS = 320
 UNIT = 416
+BODY = 400
 ZUNIT = 112
 F32 = jnp.float32
 BF16 = jnp.bfloat16
@@ -39,9 +40,9 @@
 
 
 def kernel(
-    ns_ref,
-    kw_ref,
-    mw_ref,
+    ns_in,
+    kw_in,
+    mw_in,
     design_ref,
     nuis_in,
     obs_in,
@@ -54,6 +55,9 @@
     obs_ref,
     arc_ref,
     kind_ref,
+    ns_ref,
+    kw_ref,
+    mw_ref,
     in_sem,
     dall,
     aall,
@@ -61,6 +65,7 @@
     vall,
     ahi,
     alo,
+    picks,
     tt,
     bout,
     rrel,
@@ -126,7 +131,15 @@
     small_loads = [
         pltpu.make_async_copy(src, dst, in_sem.at[k])
         for k, (src, dst) in enumerate(
-            ((nuis_in, nuis_ref), (obs_in, obs_ref), (arc_in, arc_ref), (kind_in, kind_ref))
+            (
+                (nuis_in, nuis_ref),
+                (obs_in, obs_ref),
+                (arc_in, arc_ref),
+                (kind_in, kind_ref),
+                (ns_in, ns_ref),
+                (kw_in, kw_ref),
+                (mw_in, mw_ref),
+            )
         )
     ]
     for c in range(NCHUNK):
@@ -340,6 +353,15 @@
     for k in range(7):
         send_v(k).start()
 
+    prow = iota((ROWS, CHUNK), 0)
+    pcol = iota((ROWS, CHUNK), 1)
+    pj = prow >> 3
+    py = (pj >= 10).astype(jnp.int32) + (pj >= 20).astype(jnp.int32) + (pj >= 30).astype(jnp.int32)
+    target = 80 * (prow & 7) + 20 * py + 10 * core + (pj - 10 * py)
+    for half in range(2):
+        hit = (pcol == target) if half == 0 else ((CHUNK - 1 - pcol) == target)
+        picks[half] = jnp.where(hit, 1.0, 0.0).astype(BF16)
+
     recv_x(1, xp).wait_recv()
     fwd_p(xp).start()
     recv_x(2, 7 - xm).wait_recv()
@@ -369,11 +391,6 @@
         ahi[b * OBS : (b + 1) * OBS, :] = dot(hi, sel).astype(BF16)
         alo[b * OBS : (b + 1) * OBS, :] = dot(lo, sel).astype(BF16)
 
-    prow = iota((ROWS, CHUNK), 0)
-    pcol = iota((ROWS, CHUNK), 1)
-    pj = prow >> 3
-    py = (pj >= 10).astype(jnp.int32) + (pj >= 20).astype(jnp.int32) + (pj >= 30).astype(jnp.int32)
-    target = 80 * (prow & 7) + 20 * py + 10 * core + (pj - 10 * py)
 
     for k in range(7):
         send_v(k).wait_recv()
@@ -408,10 +425,10 @@
         recv_partner(slot, 7 - x).wait_recv()
 
     for half in range(2):
-        hit = (pcol == target) if half == 0 else ((CHUNK - 1 - pcol) == target)
-        pick = jnp.where(hit, 1.0, 0.0).astype(BF16)
-        chosen = dot_t(pick, dall[x if half == 0 else 7 - x]).astype(BF16)
+        chosen = dot_t(picks[half], dall[x if half == 0 else 7 - x]).astype(BF16)
         tt[half] = (dot(chosen, ahi[...]) + dot(chosen, alo[...])).astype(BF16)
+
+    order = [pair(e, x) for e in range(4)]
 
     def put(q, val):
         for yy in range(4):
@@ -429,37 +446,64 @@
             parts.append(dot(whole[:, 128 * (4 - t) : 128 * (4 - t) + 128], rev).astype(BF16))
         return jnp.concatenate(parts, axis=1)
 
-    def y_first(q, up):
+    def y_first(q, up, rows):
         near = yp if up else ym
         far2 = (y + 2) % 4
-        return remote(bout.at[q, far2], rrel.at[q], ys1.at[q], yr1.at[q], dev(x, near, s, core))
-
-    def y_back(q, up):
+        part = pl.ds(0, rows)
+        return remote(
+            bout.at[q, far2, part],
+            rrel.at[q, part],
+            ys1.at[q],
+            yr1.at[q],
+            dev(x, near, s, core),
+        )
+
+    def y_back(q, up, rows):
         far = ym if up else yp
-        return remote(bout.at[q, far], rdir.at[q], ys2.at[q], yr2.at[q], dev(x, far, s, core))
-
-    def y_sum(q, up):
+        part = pl.ds(0, rows)
+        return remote(
+            bout.at[q, far, part],
+            rdir.at[q, part],
+            ys2.at[q],
+            yr2.at[q],
+            dev(x, far, s, core),
+        )
+
+    def y_sum(q, up, rows):
         near = yp if up else ym
-        return remote(bout.at[q, near], rsum.at[q], ys3.at[q], yr3.at[q], dev(x, near, s, core))
-
-    def y_send(q, up):
-        y_first(q, up).start()
-        y_back(q, up).start()
-
-    def y_relay(p):
-        for q, up in ((7 - p, False), (p, True)):
+        part = pl.ds(0, rows)
+        return remote(
+            bout.at[q, near, part],
+            rsum.at[q, part],
+            ys3.at[q],
+            yr3.at[q],
+            dev(x, near, s, core),
+        )
+
+    def y_parts(e):
+        p = order[e]
+        return ((7 - p, False, BODY), (p, True, UNIT if e == 0 else BODY))
+
+    def y_send(e):
+        for part in y_parts(e):
+            y_first(*part).start()
+        for part in y_parts(e):
+            y_back(*part).start()
+
+    def y_relay(e):
+        for part in y_parts(e):
+            q, up, rows = part
             near = yp if up else ym
-            y_first(q, up).wait_recv()
-            bout[q, near] = (bout[q, near].astype(F32) + rrel[q].astype(F32)).astype(BF16)
-            y_sum(q, up).start()
-
-    zero = jnp.zeros((16, 128), BF16)
-
-    def outputs(p, e):
-        for yy in range(4):
-            bout[7 - p, yy, 400:416, :] = zero
+            y_first(*part).wait_recv()
+            mine = bout[q, near, 0:rows, :].astype(F32)
+            bout[q, near, 0:rows, :] = (mine + rrel[q, 0:rows, :].astype(F32)).astype(BF16)
+            y_sum(*part).start()
+
+    def outputs(e):
+        p = order[e]
         put(7 - p, dot(tt[0], dall[7 - p]))
-        y_send(7 - p, False)
+        if e < 2:
+            y_first(*y_parts(e)[0]).start()
         if e == 0:
             put(p, jnp.where(pcol >= target, dot(tt[0], dall[p]), dot(tt[1], mirrored(7 - p))))
         else:
@@ -472,9 +516,10 @@
             def _():
                 put(p, dot(tt[1], mirrored(7 - p)))
 
-            for yy in range(4):
-                bout[p, yy, 400:416, :] = zero
-        y_send(p, True)
+        if e < 2:
+            y_first(*y_parts(e)[1]).start()
+            for part in y_parts(e):
+                y_back(*part).start()
 
     def z_copy(p, d):
         to = (s + d) % NZ
@@ -486,20 +531,25 @@
 
     zf[...] = jnp.zeros(zf.shape, F32)
 
-    def y_final(p):
-        for half, (q, up) in enumerate(((p, True), (7 - p, False))):
-            y_back(q, up).wait_recv()
-            y_sum(q, up).wait_recv()
-            fz[half] = bout[q, y].astype(F32) + rdir[q].astype(F32) + rsum[q].astype(F32)
+    def y_final(e):
+        p = order[e]
+        for part in y_parts(e):
+            q, up, rows = part
+            y_back(*part).wait_recv()
+            y_sum(*part).wait_recv()
+            total = bout[q, y, 0:rows, :].astype(F32) + rdir[q, 0:rows, :].astype(F32)
+            fz[1 - int(up), 0:rows, :] = total + rsum[q, 0:rows, :].astype(F32)
         for k in range(NZ):
             zf[k, 0:50, :] = fz[0, pl.ds(k, 50, stride=8), :]
             zf[k, 50:100, :] = fz[1, pl.ds(k, 50, stride=8), :]
-            zf[k, 100:101, :] = fz[0, 400 + k : 401 + k, :]
+            if e == 0:
+                zf[k, 100:101, :] = fz[0, 400 + k : 401 + k, :]
             zs[p, k] = zf[k].astype(BF16)
         for d in range(1, NZ):
             z_copy(p, d).start()
 
-    def z_final(p, e):
+    def z_final(e):
+        p = order[e]
         total = zs[p, s].astype(F32)
         for d in range(1, NZ):
             z_recv(p, d).wait_recv()
@@ -534,9 +584,9 @@
 
         fwd_m(pm).start()
 
-    def line(e):
+    def line(e, slots):
         p = pair(e, x)
-        if e == 1:
+        if e == 1 and 1 in slots:
 
             @pl.when((p != xp) & (p != pair(1, xp)))
             def _():
@@ -546,39 +596,47 @@
             def _():
                 recv_x(2, 7 - p).wait_recv()
 
-        for slot in (1, 2, 3):
+        for slot in slots:
             for c, upper in ((p, False), (7 - p, True)):
                 if slot == 3 or (slot == 1) == upper:
                     recv_x(slot, c).wait_recv()
                 partner(slot, c).start()
+
+    def line_end(e):
+        p = pair(e, x)
         for slot in range(4):
             recv_partner(slot, p).wait_recv()
             recv_partner(slot, 7 - p).wait_recv()
 
-    order = [pair(e, x) for e in range(4)]
-    outputs(order[0], 0)
+    outputs(0)
     relays(1)
     own_upper(3)
-    line(1)
-    outputs(order[1], 1)
-    y_relay(order[0])
+    line(1, (1, 2))
+    y_relay(0)
+    line(1, (3,))
     relays(2)
+    line_end(1)
+    outputs(1)
     relays(3)
-    line(2)
-    outputs(order[2], 2)
-    y_relay(order[1])
-    line(3)
-    outputs(order[3], 3)
-    y_final(order[0])
-    y_relay(order[2])
-    y_final(order[1])
-    y_relay(order[3])
-    z_final(order[0], 0)
-    y_final(order[2])
-    z_final(order[1], 1)
-    y_final(order[3])
-    z_final(order[2], 2)
-    z_final(order[3], 3)
+    line(2, (1, 2, 3))
+    line_end(2)
+    outputs(2)
+    y_final(0)
+    y_relay(1)
+    y_send(2)
+    line(3, (1, 2, 3))
+    line_end(3)
+    outputs(3)
+    y_final(1)
+    y_relay(2)
+    y_send(3)
+    z_final(0)
+    y_final(2)
+    y_relay(3)
+    z_final(1)
+    y_final(3)
+    z_final(2)
+    z_final(3)
 
     for c in range(NCHUNK):
         own_p(c).wait_send()
@@ -593,10 +651,11 @@
         send_a(slot).wait_send()
     for k in range(7):
         send_v(k).wait_send()
-    for q in range(NCHUNK):
-        y_first(q, q < 4).wait_send()
-        y_back(q, q < 4).wait_send()
-        y_sum(q, q < 4).wait_send()
+    for e in range(4):
+        for part in y_parts(e):
+            y_first(*part).wait_send()
+            y_back(*part).wait_send()
+            y_sum(*part).wait_send()
     for p in range(4):
         for d in range(1, NZ):
             z_copy(p, d).wait_send()
@@ -604,20 +663,23 @@
 
 def on_device(design, nuisance, observed, arc_of_row, nuis_size, kinds, kind_weight, mission_weight):
     vmem = pl.BlockSpec(memory_space=pltpu.VMEM)
-    smem = pl.BlockSpec(memory_space=pltpu.SMEM)
     dma = pltpu.SemaphoreType.DMA
     scratch = [
         pltpu.VMEM((OBS, 128), BF16),
         pltpu.VMEM((1, OBS), F32),
         pltpu.VMEM((1, OBS), jnp.int32),
         pltpu.VMEM((1, OBS), jnp.int32),
-        dma((4,)),
+        pltpu.SMEM((2,), jnp.int32),
+        pltpu.SMEM((8,), F32),
+        pltpu.SMEM((1,), F32),
+        dma((7,)),
         pltpu.VMEM((NCHUNK, 640, CHUNK), BF16),
         pltpu.VMEM((640, 128), F32),
         pltpu.VMEM((4, 16, 128), F32),
         pltpu.VMEM((7, 16, 128), F32),
         pltpu.VMEM((640, 640), BF16),
         pltpu.VMEM((640, 640), BF16),
+        pltpu.VMEM((2, ROWS, 640), BF16),
         pltpu.VMEM((2, ROWS, 640), BF16),
         pltpu.VMEM((NCHUNK, 4, UNIT, 128), BF16),
         pltpu.VMEM((NCHUNK, UNIT, 128), BF16),
@@ -658,7 +720,7 @@
             jax.ShapeDtypeStruct((1, 20), F32),
             jax.ShapeDtypeStruct((1, 10), F32),
         ),
-        in_specs=[smem] * 3 + [pl.BlockSpec(memory_space=pl.ANY)] * 5,
+        in_specs=[pl.BlockSpec(memory_space=pl.ANY)] * 8,
         out_specs=(vmem, vmem, vmem),
         scratch_shapes=scratch,
         compiler_params=pltpu.CompilerParams(

time: 79.9 us -> 76.3 us (0.955)
  the two profiles are of different devices: /device:TPU:6 before, /device:TPU:1 now
where the time goes in v3:
time: 76.3 us; the launch traced here: 76.2 us
  Pallas kernels  72 us (94%)
  local copies, waits for them, and re-layouts  2.9 us (4%)
  between operations  1.3 us (2%)
    pallas_call x1, Pallas kernels, on_device(): pl.pallas_call(kernel, out_shape=(jax.ShapeDtypeStruct((10, WIDTH), F32),...  72 us
    unnamed x7, local copies, waits for them, and re-layouts  2.9 us

profile of v3, /device:TPU:1, one launch (start us, length us, event | category | flops | bytes accessed | tf_op | source)
XLA Modules:
  0.0 76.2 jit_solution(9988011894587292804)
XLA Ops:
  1.3 72.0 %shard_map.103 = (f32[10,5120]{1,0:T(8,128)}, f32[1,20]{1,0:T(1,128)}, f32[1,10]{1,0:T(1,128)}) custom-call(s32[2]{0:T(128)} %ns_in.1, f32[8]{0:T(128)} %kw_in.1, f32[1]{0:T(128)S(6)} %copy.14.mw_in, bf16[80,5120]{1,0:T(8,128)(2,1)} %design_ref.1, bf16[80,128]{1,0:T(8,128)(2,1)} %nuis_in.1, f32[1,80]{1,0:T(1,128)} %bitcast.5, s32[1,80]{1,0:T(1,128)} %bitcast.6, ...), custom_call_target="tpu_custom_call" | custom-call | tf_op jit(solution)/shard_map/pallas_call | solution.py:716
  73.3 0.0 copy-start.1
  73.3 1.7 %copy.15 = f32[10,5120]{1,0:T(8,128)} copy(f32[10,5120]{1,0:T(8,128)} %get-tuple-element.12) | data formatting | bytes 409600
  75.0 0.0 copy-done.1
  75.0 0.0 copy-start
  75.0 0.5 copy.16
  75.5 0.2 copy-done
  75.7 0.5 copy.17
Async XLA Ops:
  73.3 1.7 %copy-start.1 = (f32[1,20]{1,0:T(1,128)S(1)}, f32[1,20]{1,0:T(1,128)}, u32[]{:S(2)}) copy-start(f32[1,20]{1,0:T(1,128)} %get-tuple-element.7) | copy-start | bytes 244
  75.0 0.7 copy-start

commit v4 on v3

--- a/solution.py
+++ b/solution.py
@@ -370,7 +370,6 @@
     own_upper(1)
     own_lower(2)
     own_upper(2)
-    own_lower(3)
 
     for slot in (1, 2):
         for c in (x, 7 - x):
@@ -426,7 +425,10 @@
 
     for half in range(2):
         chosen = dot_t(picks[half], dall[x if half == 0 else 7 - x]).astype(BF16)
-        tt[half] = (dot(chosen, ahi[...]) + dot(chosen, alo[...])).astype(BF16)
+        for c0, c1, r0, r1 in ((0, 256, 0, 384), (256, 512, 128, 640), (512, 640, 384, 640)):
+            left = chosen[:, r0:r1]
+            part = dot(left, ahi[r0:r1, c0:c1]) + dot(left, alo[r0:r1, c0:c1])
+            tt[half, :, c0:c1] = part.astype(BF16)
 
     order = [pair(e, x) for e in range(4)]
 
@@ -608,22 +610,22 @@
             recv_partner(slot, p).wait_recv()
             recv_partner(slot, 7 - p).wait_recv()
 
+    relays(1)
+    own_lower(3)
+    own_upper(3)
     outputs(0)
-    relays(1)
-    own_upper(3)
-    line(1, (1, 2))
+    line(1, (1, 2, 3))
+    relays(2)
     y_relay(0)
-    line(1, (3,))
-    relays(2)
     line_end(1)
     outputs(1)
     relays(3)
     line(2, (1, 2, 3))
+    y_relay(1)
     line_end(2)
     outputs(2)
+    y_send(2)
     y_final(0)
-    y_relay(1)
-    y_send(2)
     line(3, (1, 2, 3))
     line_end(3)
     outputs(3)

time: 76.3 us -> 74.5 us (0.976)
  the two profiles are of different devices: /device:TPU:1 before, /device:TPU:6 now
where the time goes in v4:
time: 74.5 us; the launch traced here: 73.7 us
  Pallas kernels  69.5 us (93%)
  local copies, waits for them, and re-layouts  2.9 us (4%)
  between operations  1.3 us (2%)
    pallas_call x1, Pallas kernels, on_device(): pl.pallas_call(kernel, out_shape=(jax.ShapeDtypeStruct((10, WIDTH), F32),...  69.5 us
    unnamed x7, local copies, waits for them, and re-layouts  2.9 us

profile of v4, /device:TPU:6, one launch (start us, length us, event | category | flops | bytes accessed | tf_op | source)
XLA Modules:
  0.0 73.7 jit_solution(16175757653169505996)
XLA Ops:
  1.3 69.5 %shard_map.103 = (f32[10,5120]{1,0:T(8,128)}, f32[1,20]{1,0:T(1,128)}, f32[1,10]{1,0:T(1,128)}) custom-call(s32[2]{0:T(128)} %ns_in.1, f32[8]{0:T(128)} %kw_in.1, f32[1]{0:T(128)S(6)} %copy.14.mw_in, bf16[80,5120]{1,0:T(8,128)(2,1)} %design_ref.1, bf16[80,128]{1,0:T(8,128)(2,1)} %nuis_in.1, f32[1,80]{1,0:T(1,128)} %bitcast.5, s32[1,80]{1,0:T(1,128)} %bitcast.6, ...), custom_call_target="tpu_custom_call" | custom-call | tf_op jit(solution)/shard_map/pallas_call | solution.py:718
  70.8 0.0 copy-start.1
  70.8 1.7 %copy.15 = f32[10,5120]{1,0:T(8,128)} copy(f32[10,5120]{1,0:T(8,128)} %get-tuple-element.12) | data formatting | bytes 409600
  72.6 0.0 copy-done.1
  72.6 0.0 copy-start
  72.6 0.5 copy.16
  73.1 0.2 copy-done
  73.2 0.5 copy.17
Async XLA Ops:
  70.8 1.7 %copy-start.1 = (f32[1,20]{1,0:T(1,128)S(1)}, f32[1,20]{1,0:T(1,128)}, u32[]{:S(2)}) copy-start(f32[1,20]{1,0:T(1,128)} %get-tuple-element.7) | copy-start | bytes 244
  72.6 0.7 copy-start

commit v5 on v4

--- a/solution.py
+++ b/solution.py
@@ -621,12 +621,13 @@
     outputs(1)
     relays(3)
     line(2, (1, 2, 3))
+    line(3, (1, 2))
     y_relay(1)
     line_end(2)
     outputs(2)
     y_send(2)
     y_final(0)
-    line(3, (1, 2, 3))
+    line(3, (3,))
     line_end(3)
     outputs(3)
     y_final(1)

time: 74.5 us -> 74.5 us (level)
  no operation moved by 1% of the time
where the time goes in v5:
time: 74.5 us; the launch traced here: 73.8 us
  Pallas kernels  69.6 us (93%)
  local copies, waits for them, and re-layouts  2.9 us (4%)
  between operations  1.3 us (2%)
    pallas_call x1, Pallas kernels, on_device(): pl.pallas_call(kernel, out_shape=(jax.ShapeDtypeStruct((10, WIDTH), F32),...  69.6 us
    unnamed x7, local copies, waits for them, and re-layouts  2.9 us

profile of v5, /device:TPU:6, one launch (start us, length us, event | category | flops | bytes accessed | tf_op | source)
XLA Modules:
  0.0 73.8 jit_solution(16116919081269477443)
XLA Ops:
  1.3 69.6 %shard_map.103 = (f32[10,5120]{1,0:T(8,128)}, f32[1,20]{1,0:T(1,128)}, f32[1,10]{1,0:T(1,128)}) custom-call(s32[2]{0:T(128)} %ns_in.1, f32[8]{0:T(128)} %kw_in.1, f32[1]{0:T(128)S(6)} %copy.14.mw_in, bf16[80,5120]{1,0:T(8,128)(2,1)} %design_ref.1, bf16[80,128]{1,0:T(8,128)(2,1)} %nuis_in.1, f32[1,80]{1,0:T(1,128)} %bitcast.5, s32[1,80]{1,0:T(1,128)} %bitcast.6, ...), custom_call_target="tpu_custom_call" | custom-call | tf_op jit(solution)/shard_map/pallas_call | solution.py:719
  70.9 0.0 copy-start.1
  70.9 1.7 %copy.15 = f32[10,5120]{1,0:T(8,128)} copy(f32[10,5120]{1,0:T(8,128)} %get-tuple-element.12) | data formatting | bytes 409600
  72.7 0.0 copy-done.1
  72.7 0.0 copy-start
  72.7 0.5 copy.16
  73.2 0.2 copy-done
  73.3 0.5 copy.17
Async XLA Ops:
  70.9 1.7 %copy-start.1 = (f32[1,20]{1,0:T(1,128)S(1)}, f32[1,20]{1,0:T(1,128)}, u32[]{:S(2)}) copy-start(f32[1,20]{1,0:T(1,128)} %get-tuple-element.7) | copy-start | bytes 244
  72.7 0.7 copy-start
